TPU v7x, 32 devices: a whole 2x2x4 slice. The times are simulated.
32 devices in a mesh: rows: 8 (over z, y), groups: 4 (over x, core).
Axes of the slice: x: 2, y: 2, z: 4, core: 2. Of those that a mesh axis runs over, the one named last changes fastest.
Arguments:
- basis: bfloat16 [8, 131072, 128], P(None, ('rows', 'groups')), may hold values from -6 to 6
- image: bfloat16 [8, 131072, 128], P(None, ('rows', 'groups')), may hold values from -6 to 6
- selection: int32 [8, 64], replicated, may hold values from 0 to 127, all different within a row
Outputs:
- rotated: bfloat16 [8, 131072, 128], P(None, ('rows', 'groups'))
Inputs may be any that keep to these rules, and one draw needn't show every extreme that they name: Each row of selection names 64 different columns.
All inputs are finite; a program needn't handle non-finite values.
Results may differ from a plain program's by a relative error of at most 0.005.
Values may be sent and summed in bfloat16 or wider, within the bound.
A program may use at most 128 MiB of HBM per device.

v0:
```python
import jax
import jax.numpy as jnp
from jax import lax
from jax.sharding import PartitionSpec as P

ITERS = 3


def small_solve(grams, chosen, total_rows):
    gram_s, cross, gram_f = (grams[0], grams[1], grams[2])
    width = gram_s.shape[0]
    coeffs = (jnp.arange(width, dtype=jnp.int32)[:, None] == chosen[None, :]).astype(jnp.float32)
    factor = jnp.linalg.cholesky(gram_f)
    for step in range(ITERS):
        moved = jnp.dot(cross.T, coeffs, precision=lax.Precision.HIGHEST)
        halfway = lax.linalg.triangular_solve(factor, moved, left_side=True, lower=True)
        solved = lax.linalg.triangular_solve(
            factor, halfway, left_side=True, lower=True, transpose_a=True
        )
        metric = (
            jnp.dot(
                solved.T,
                jnp.dot(gram_s, solved, precision=lax.Precision.HIGHEST),
                precision=lax.Precision.HIGHEST,
            )
            / total_rows
        )
        lower = jnp.linalg.cholesky(metric)
        coeffs = lax.linalg.triangular_solve(
            lower, solved, left_side=False, lower=True, transpose_a=True
        )
    return coeffs


def on_device(basis, image, selection):
    total_rows = basis.shape[1] * lax.axis_size("rows") * lax.axis_size("groups")
    gram_s = jnp.einsum("srk,srl->skl", basis, basis, preferred_element_type=jnp.float32)
    cross = jnp.einsum("srk,srl->skl", basis, image, preferred_element_type=jnp.float32)
    gram_f = jnp.einsum("srk,srl->skl", image, image, preferred_element_type=jnp.float32)
    partial_grams = jnp.stack([gram_s, cross, gram_f], axis=1)
    solver = jax.vmap(lambda grams, chosen: small_solve(grams, chosen, total_rows))
    shares = lax.psum_scatter(partial_grams, "groups", scatter_dimension=0, tiled=True)
    summed = lax.psum(shares, "rows")
    grams = summed
    count = shares.shape[0]
    start = lax.axis_index("groups") * count
    mine = lax.dynamic_slice_in_dim(selection, start, count, 0)
    local_coeffs = solver(grams, mine).astype(jnp.bfloat16)
    narrow = lax.all_gather(local_coeffs, "groups", axis=0, tiled=True)
    first = jnp.einsum("srk,skj->srj", basis, narrow, preferred_element_type=jnp.float32)
    second = jnp.einsum("srk,skj->srj", image, narrow, preferred_element_type=jnp.float32)
    return jnp.concatenate([first, second], axis=2).astype(jnp.bfloat16)


def solution(mesh):
    in_specs = (P(None, ("rows", "groups"), None), P(None, ("rows", "groups"), None), P())
    out_specs = P(None, ("rows", "groups"), None)
    return jax.shard_map(
        on_device, mesh=mesh, in_specs=in_specs, out_specs=out_specs, check_vma=False
    )
```

profile of v0, /device:TPU:0, one launch (start us, length us, event | category | flops | bytes accessed | tf_op | source)
XLA Modules:
  0.0 317.1 jit_solution(13355528183286181943)
XLA Ops:
  6.5 8.5 %convolution_bitcast_fusion.2 = f32[8,1,128,128]{3,2,0,1:T(8,128)S(1)} fusion(bf16[8,4096,128]{2,1,0:T(8,128)(2,1)} %param.10), kind=kOutput, calls=%fused_computation.8 | convolution fusion | flops 1073741824 | bytes 8912896 | tf_op jit(solution)/shard_map/srk,srl->skl/dot_general | solution.py:37
  15.0 5.9 %convolution_bitcast_fusion.1 = f32[8,1,128,128]{3,2,0,1:T(8,128)S(1)} fusion(bf16[8,4096,128]{2,1,0:T(8,128)(2,1)} %param.10, bf16[8,4096,128]{2,1,0:T(8,128)(2,1)S(1)} %copy-done.1), kind=kOutput, calls=%fused_computation.7 | convolution fusion | flops 1073741824 | bytes 17301504 | tf_op jit(solution)/shard_map/srk,srl->skl/dot_general | solution.py:38
  21.0 2.6 convolution_bitcast_fusion
  23.7 1.6 copy.51
  26.9 44.3 %all-reduce.6.cloned.1.call-done = f32[8,3,128,128]{2,3,0,1:T(8,128)} async-done(((f32[8,3,128,128]{2,3,0,1:T(8,128)}), f32[8,3,128,128]{2,3,0,1:T(8,128)}) %all-reduce.6.cloned.1.call-update) | async-done | bytes 1572880
  71.1 1.8 constant_dynamic-slice_fusion
  73.0 73.3 %all-reduce.4.cloned.1.call-done = f32[2,3,128,128]{2,3,0,1:T(8,128)} async-done(((f32[2,3,128,128]{2,3,0,1:T(8,128)}), f32[2,3,128,128]{2,3,0,1:T(8,128)}) %all-reduce.4.cloned.1.call-update) | async-done | bytes 393232 | tf_op jit(solution)/shard_map/psum | solution.py:43
  148.3 23.5 %custom-call.16 = f32[2,128,128]{2,1,0:T(8,128)S(1)} custom-call(f32[2,128,128]{2,1,0:T(8,128)S(1)} %fusion.3), custom_call_target="Cholesky" | custom-call | tf_op jit(solution)/shard_map/vmap(jit(cholesky))/cholesky | solution.py:13
  172.0 19.7 %custom-call.34 = f32[2,1,128,128]{2,3,1,0:T(8,128)S(1)} custom-call(f32[2,1,128,128]{3,2,1,0:T(8,128)S(1)} %select_bitcast_fusion), custom_call_target="InvertDiagBlocksLowerTriangular" | custom-call | tf_op jit(solution)/shard_map/vmap()/triangular_solve/custom-call.3 | solution.py:17
  191.7 1.2 fusion.18
  195.0 11.7 %custom-call.27 = f32[2,64,64]{2,1,0:T(8,128)S(1)} custom-call(f32[2,64,64]{2,1,0:T(8,128)S(1)} %fusion.27), custom_call_target="Cholesky" | custom-call | tf_op jit(solution)/shard_map/vmap(jit(cholesky))/cholesky | solution.py:28
  206.9 9.8 %custom-call.28 = f32[2,1,64,64]{2,3,1,0:T(8,128)S(1)} custom-call(f32[2,1,64,64]{3,2,1,0:T(8,128)S(1)} %select_bitcast_fusion.3), custom_call_target="InvertDiagBlocksLowerTriangular" | custom-call | tf_op jit(solution)/shard_map/vmap()/triangular_solve/custom-call.4 | solution.py:29
  217.1 1.3 fusion.17
  219.0 1.2 fusion.20
  220.5 11.7 %custom-call.31 = f32[2,64,64]{2,1,0:T(8,128)S(1)} custom-call(f32[2,64,64]{2,1,0:T(8,128)S(1)} %fusion.25), custom_call_target="Cholesky" | custom-call | tf_op jit(solution)/shard_map/vmap(jit(cholesky))/cholesky | solution.py:28
  232.4 10.0 %custom-call.32 = f32[2,1,64,64]{2,3,1,0:T(8,128)S(1)} custom-call(f32[2,1,64,64]{3,2,1,0:T(8,128)S(1)} %select_bitcast_fusion.2), custom_call_target="InvertDiagBlocksLowerTriangular" | custom-call | tf_op jit(solution)/shard_map/vmap()/triangular_solve/custom-call.4 | solution.py:29
  242.8 1.3 fusion.16
  246.2 11.7 %custom-call.35 = f32[2,64,64]{2,1,0:T(8,128)S(1)} custom-call(f32[2,64,64]{2,1,0:T(8,128)S(1)} %fusion.23), custom_call_target="Cholesky" | custom-call | tf_op jit(solution)/shard_map/vmap(jit(cholesky))/cholesky | solution.py:28
  258.1 9.8 %custom-call.36 = f32[2,1,64,64]{2,3,1,0:T(8,128)S(1)} custom-call(f32[2,1,64,64]{3,2,1,0:T(8,128)S(1)} %select_bitcast_fusion.1), custom_call_target="InvertDiagBlocksLowerTriangular" | custom-call | tf_op jit(solution)/shard_map/vmap()/triangular_solve/custom-call.4 | solution.py:29
  268.3 5.4 %all_gather.3 = bf16[8,128,64]{1,2,0:T(8,128)(2,1)S(1)} all-gather(bf16[2,128,64]{1,2,0:T(8,128)(2,1)S(1)} %fusion.2), channel_id=1, replica_groups=mesh['rows'=8,'groups'=4] {'groups'}, dimensions={0}, use_global_device_ids=true | all-gather | bytes 163840 | tf_op jit(solution)/shard_map/all_gather | solution.py:49
  273.7 8.4 %fusion.1 = bf16[8,4096,64]{1,2,0:T(8,128)(2,1)} fusion(bf16[8,128,64]{1,2,0:T(8,128)(2,1)S(1)} %all_gather.3, bf16[8,4096,128]{2,1,0:T(8,128)(2,1)} %param.11), kind=kOutput, calls=%fused_computation.4 | convolution fusion | flops 538968064 | bytes 12713984 | tf_op jit(solution)/shard_map/srk,skj->srj/dot_general | solution.py:51
  282.1 8.4 %fusion = bf16[8,4096,64]{1,2,0:T(8,128)(2,1)} fusion(bf16[8,128,64]{1,2,0:T(8,128)(2,1)S(1)} %all_gather.3, bf16[8,4096,128]{2,1,0:T(8,128)(2,1)} %param.10), kind=kOutput, calls=%fused_computation.3 | convolution fusion | flops 538968064 | bytes 12713984 | tf_op jit(solution)/shard_map/srk,skj->srj/dot_general | solution.py:50
  290.5 7.8 %pad_maximum_fusion = bf16[8,4096,128]{1,2,0:T(8,128)(2,1)} fusion(bf16[8,4096,64]{1,2,0:T(8,128)(2,1)} %fusion.1, bf16[8,4096,64]{1,2,0:T(8,128)(2,1)} %fusion), kind=kLoop, calls=%fused_computation | loop fusion | flops 16777216 | bytes 16777216 | tf_op jit(solution)/shard_map/concatenate | solution.py:52
  298.3 11.9 %copy.79 = bf16[8,4096,128]{2,1,0:T(8,128)(2,1)} copy(bf16[8,4096,128]{1,2,0:T(8,128)(2,1)} %pad_maximum_fusion) | data formatting | bytes 16777216 | tf_op jit(solution)/shard_map/concatenate | solution.py:52
  (52 shorter events, 10.0 us)
Async XLA Ops:
  6.5 66.4 %copy-start = (s32[8,64]{1,0:T(8,128)S(1)}, s32[8,64]{1,0:T(8,128)}, u32[]{:S(2)}) copy-start(s32[8,64]{1,0:T(8,128)} %param.12) | copy-start | bytes 6148
  6.5 64.6 %all-reduce.6.cloned.1.call-start = ((), (), s32[]{:S(2)}) async-start(), calls=%async_computation.1 | async-start | bytes 3145728
  6.5 8.5 %copy-start.1 = (bf16[8,4096,128]{2,1,0:T(8,128)(2,1)S(1)}, bf16[8,4096,128]{2,1,0:T(8,128)(2,1)}, u32[]{:S(2)}) copy-start(bf16[8,4096,128]{2,1,0:T(8,128)(2,1)} %param.11) | copy-start | bytes 25165828
  21.0 4.6 %copy-start.2 = (u32[32]{0:T(128)S(1)}, u32[32]{0:T(128)}, u32[]{:S(2)}) copy-start(u32[32]{0:T(128)} %constant.92) | copy-start | bytes 388
  25.4 120.9 %all-reduce.4.cloned.1.call-start = ((), (), s32[]{:S(2)}) async-start(), calls=%async_computation | async-start | bytes 786432 | tf_op jit(solution)/shard_map/psum | solution.py:43
Sparse Core Ops, SparseCore 0:
  25.5 45.6 all-reduce.5
  74.5 71.7 all-reduce.3
where the time goes:
time: 318 us; the launch traced here: 317 us
  other arithmetic  118 us (37%)
  waiting for transfers between devices  118 us (37%)
  matrix products  44.3 us (14%)
  local copies, waits for them, and re-layouts  17.2 us (5%)
  between operations  14.4 us (5%)
  blocking collectives  5.42 us (2%)
    psum x1, waiting for transfers between devices, on_device(): summed = lax.psum(shares, 'rows')  73.3 us
    unnamed x3, waiting for transfers between devices  44.3 us
    another operation x10, other arithmetic, small_solve(): lower = jnp.linalg.cholesky(metric)  35.6 us
    another operation x7, other arithmetic, small_solve(): lax.linalg.triangular_solve(lower, solved, left_side=False, lower=True, t...  30 us
    another operation x4, other arithmetic, small_solve(): factor = jnp.linalg.cholesky(gram_f)  23.6 us
    another operation x3, other arithmetic, small_solve(): lax.linalg.triangular_solve(factor, halfway, left_side=True, lower=True,...  19.8 us
    concatenate x1, local copies, waits for them, and re-layouts, on_device(): return jnp.concatenate([first, second], axis=2).astype(jnp.bfloat16)  11.9 us
    dot_general x1, matrix products, on_device(): jnp.einsum('srk,srl->skl', basis, basis, preferred_element_type=jnp.float32)  8.47 us
  transfers between devices with their start and end apart: 2, of which 2 were waited for; matrix products, arithmetic and copies ran while one was open for 0% of the time, Pallas kernels for 0%

commit v1 on v0

v1 whole, which is shorter than its diff:
```python
import functools

import jax
import jax.numpy as jnp
from jax import lax
from jax.experimental import pallas as pl
from jax.experimental.pallas import tpu as pltpu
from jax.sharding import PartitionSpec as P

ITERS = 3
PANEL = 8
MESH = pl.DeviceIdType.MESH
NT = (((1,), (1,)), ((), ()))
TN = (((0,), (0,)), ((), ()))
HIGHEST = lax.Precision.HIGHEST


def exact_dot(a, b, dims=(((1,), (0,)), ((), ()))):
    return lax.dot_general(a, b, dims, precision=HIGHEST, preferred_element_type=jnp.float32)


def panel_rows(rows, first, forward):
    lanes = rows.shape[1]
    place = lax.broadcasted_iota(jnp.int32, (PANEL, 128), 0)
    wide = lax.broadcasted_iota(jnp.int32, (PANEL, lanes), 0)
    cols = [
        jnp.broadcast_to(rows[:, first + k : first + k + 1], (PANEL, 128)) for k in range(PANEL)
    ]
    full = rows
    lower = rows
    scales = []
    for j in range(PANEL):
        pivot = jnp.broadcast_to(cols[j][j : j + 1, :], (PANEL, 128))
        inv = 1.0 / pivot
        inv_wide = jnp.concatenate([inv] * (lanes // 128), axis=1)
        col_wide = jnp.concatenate([cols[j]] * (lanes // 128), axis=1)
        unit = jnp.broadcast_to(full[j : j + 1, :], full.shape) * inv_wide
        if forward:
            step = jnp.broadcast_to(lower[j : j + 1, :], lower.shape) * inv_wide
            lower = jnp.where(wide > j, lower - col_wide * step, lower)
            scales.append(pivot)
        full = jnp.where(wide == j, unit, full - col_wide * unit)
        for k in range(j + 1, PANEL):
            part = jnp.broadcast_to(cols[k][j : j + 1, :], (PANEL, 128)) * inv
            cols[k] = jnp.where(place == j, part, cols[k] - cols[j] * part)
    if not forward:
        return full, None
    pivots = scales[0]
    for j in range(1, PANEL):
        pivots = jnp.where(place == j, scales[j], pivots)
    root = lax.rsqrt(pivots)
    return full, lower * jnp.concatenate([root] * (lanes // 128), axis=1)


def solve_spd(work):
    n, lanes = work.shape
    for p in range(n // PANEL):
        first = p * PANEL
        full, _ = panel_rows(work[first : first + PANEL], first, False)
        moved = work
        for k in range(PANEL):
            moved = moved - work[:, first + k : first + k + 1] * full[k : k + 1, :]
        pieces = [moved[:first], full, moved[first + PANEL :]]
        work = jnp.concatenate([x for x in pieces if x.shape[0]], axis=0)
    return work[:, 128:]


def whiten(work):
    n, lanes = work.shape
    out = []
    for p in range(n // PANEL):
        first = p * PANEL
        full, lower = panel_rows(work[:PANEL], first, True)
        out.append(lower[:, 128:])
        work = work[PANEL:]
        if work.shape[0]:
            moved = work
            for k in range(PANEL):
                moved = moved - work[:, first + k : first + k + 1] * full[k : k + 1, :]
            work = moved
    return jnp.concatenate(out, axis=0)


def small_solve(gram_s, cross, gram_f, start, total_rows):
    width = gram_s.shape[0]
    keep = start.shape[0]
    across = solve_spd(jnp.concatenate([gram_f, cross.T], axis=1))
    turned = across.T
    coeffs = start
    for step in range(ITERS):
        solved = exact_dot(coeffs, turned)
        metric = exact_dot(exact_dot(solved, gram_s), solved, NT) / total_rows
        pad = jnp.zeros((keep, 128 - keep), jnp.float32)
        coeffs = whiten(jnp.concatenate([metric, pad, solved], axis=1))
    return coeffs


def pack(gram, width):
    gram_s = gram[:width, :width]
    gram_f = gram[width:, width:]
    row = lax.broadcasted_iota(jnp.int32, (width, width), 0)
    col = lax.broadcasted_iota(jnp.int32, (width, width), 1)
    mixed = jnp.where(row < col, gram_s, gram_f)
    diag = jnp.sum(jnp.where(row == col, gram_s, 0.0), axis=0, keepdims=True)
    return gram[:width, width:], mixed, jnp.broadcast_to(diag, (8, width))


def unpack(packed, width):
    cross = packed[:width]
    mixed = packed[width : 2 * width]
    diag = packed[2 * width : 2 * width + 1]
    row = lax.broadcasted_iota(jnp.int32, (width, width), 0)
    col = lax.broadcasted_iota(jnp.int32, (width, width), 1)
    turned = mixed.T
    gram_s = jnp.where(row < col, mixed, jnp.where(row > col, turned, diag))
    gram_f = jnp.where(row < col, turned, mixed)
    return gram_s, cross, gram_f


def coeff_kernel(
    sizes, total_rows, basis, image, chosen, out, shared, grams, got1, got2, got3, got4, sends, recvs, csend, crecv
):
    n_rows, n_groups = sizes
    nsys = grams.shape[0]
    width = basis.shape[2]
    inner = nsys // n_groups
    depth = n_rows // inner
    n_x = n_groups // 2
    step = pl.program_id(0)
    me_r = lax.axis_index("rows")
    me_g = lax.axis_index("groups")
    z, y = me_r // inner, lax.rem(me_r, inner)
    x, c = me_g // 2, lax.rem(me_g, 2)
    barrier = pltpu.get_barrier_semaphore()
    peers = n_rows * n_groups

    def nth_peer(i):
        other = lax.rem(me_r * n_groups + me_g + i, peers)
        return (other // n_groups, lax.rem(other, n_groups))

    @pl.when(step == 0)
    def _():
        def greet(i, carry):
            pl.semaphore_signal(barrier, inc=1, device_id=nth_peer(i), device_id_type=MESH)
            return carry

        lax.fori_loop(1, peers, greet, 0)

    both = jnp.concatenate([basis[0], image[0]], axis=1)
    gram = lax.dot_general(both, both, TN, preferred_element_type=jnp.float32)
    cross, mixed, diag = pack(gram, width)
    grams[step, 0:width, :] = cross
    grams[step, width : 2 * width, :] = mixed
    grams[step, 2 * width :, :] = diag

    @pl.when(step == nsys - 1)
    def _():
        pl.semaphore_wait(barrier, peers - 1)
        base = 0
        count = nsys
        slot = 0
        for size, at, spot, got in (
            (2, c, lambda k: (me_r, me_g + k - c), got1),
            (n_x, x, lambda k: (me_r, me_g + 2 * (k - x)), got2),
            (inner, y, lambda k: (me_r + k - y, me_g), got3),
        ):
            if size == 1:
                continue
            count = count // size
            copies = []
            for d in range(1, size):
                k = lax.rem(at + d, size)
                copy = pltpu.make_async_remote_copy(
                    src_ref=grams.at[pl.ds(base + k * count, count)],
                    dst_ref=got.at[pl.ds((d - 1) * count, count)],
                    send_sem=sends.at[slot],
                    recv_sem=recvs.at[slot],
                    device_id=spot(k),
                    device_id_type=MESH,
                )
                copy.start()
                copies.append(copy)
                slot += 1
            base = base + at * count
            for d, copy in enumerate(copies):
                copy.wait()
                grams[pl.ds(base, count)] += got[pl.ds(d * count, count)]
        mine = base
        root = lax.rem(2 * c + x + y, depth)

        @pl.when(z != root)
        def _():
            copy = pltpu.make_async_remote_copy(
                src_ref=grams.at[mine],
                dst_ref=got4.at[lax.rem(z - root + depth, depth) - 1],
                send_sem=sends.at[slot],
                recv_sem=recvs.at[slot + lax.rem(z - root + depth, depth) - 1],
                device_id=(root * inner + y, me_g),
                device_id_type=MESH,
            )
            copy.start()
            copy.wait_send()

        @pl.when(z == root)
        def _():
            total = grams[mine]
            for k in range(depth - 1):
                pltpu.make_async_remote_copy(
                    src_ref=grams.at[mine],
                    dst_ref=got4.at[k],
                    send_sem=sends.at[slot],
                    recv_sem=recvs.at[slot + k],
                    device_id=(me_r, me_g),
                    device_id_type=MESH,
                ).wait_recv()
                total = total + got4[k]
            gram_s, cross_s, gram_f = unpack(total, width)
            picked = chosen[pl.ds(mine, 1), :]
            row = lax.broadcasted_iota(jnp.int32, (width, picked.shape[1]), 0)
            start = (row == picked).astype(jnp.float32).T
            coeffs = small_solve(gram_s, cross_s, gram_f, start, total_rows)
            shared[pl.ds(mine, 1)] = coeffs.astype(jnp.bfloat16)[None]

            def share(i):
                return pltpu.make_async_remote_copy(
                    src_ref=shared.at[mine],
                    dst_ref=shared.at[mine],
                    send_sem=csend.at[i],
                    recv_sem=crecv.at[mine],
                    device_id=nth_peer(i),
                    device_id_type=MESH,
                )

            def send(i, carry):
                share(i).start()
                return carry

            def sent(i, carry):
                share(i).wait_send()
                return carry

            lax.fori_loop(1, peers, send, 0)
            lax.fori_loop(1, peers, sent, 0)

        for s in range(nsys):

            @pl.when(jnp.logical_or(z != root, mine != s))
            def _():
                pltpu.make_async_remote_copy(
                    src_ref=shared.at[s],
                    dst_ref=shared.at[s],
                    send_sem=csend.at[0],
                    recv_sem=crecv.at[s],
                    device_id=(me_r, me_g),
                    device_id_type=MESH,
                ).wait_recv()

        out[...] = shared[...]


def rotate_kernel(basis, image, coeffs, out):
    narrow = coeffs[0]
    first = lax.dot_general(basis[0], narrow, NT, preferred_element_type=jnp.float32)
    second = lax.dot_general(image[0], narrow, NT, preferred_element_type=jnp.float32)
    out[0] = jnp.concatenate([first, second], axis=1).astype(out.dtype)


def on_device(n_rows, n_groups, basis, image, selection):
    nsys, local, width = basis.shape
    keep = selection.shape[1]
    peers = n_rows * n_groups
    total_rows = local * peers
    inner = nsys // n_groups
    depth = n_rows // inner
    n_x = n_groups // 2
    hops = n_x + max(inner - 1, 1)
    tall = 2 * width + 8
    whole = pl.BlockSpec((1, local, width), lambda s: (s, 0, 0))
    coeffs = pl.pallas_call(
        functools.partial(coeff_kernel, (n_rows, n_groups), total_rows),
        grid=(nsys,),
        in_specs=[whole, whole, pl.BlockSpec(memory_space=pltpu.VMEM)],
        out_specs=pl.BlockSpec(memory_space=pltpu.VMEM),
        out_shape=jax.ShapeDtypeStruct((nsys, keep, width), jnp.bfloat16),
        scratch_shapes=[
            pltpu.VMEM((nsys, keep, width), jnp.bfloat16),
            pltpu.VMEM((nsys, tall, width), jnp.float32),
            pltpu.VMEM((nsys // 2, tall, width), jnp.float32),
            pltpu.VMEM(((n_x - 1) * nsys // n_groups, tall, width), jnp.float32),
            pltpu.VMEM((max(inner - 1, 1), tall, width), jnp.float32),
            pltpu.VMEM((depth - 1, tall, width), jnp.float32),
            pltpu.SemaphoreType.DMA((hops + 1,)),
            pltpu.SemaphoreType.DMA((hops + depth - 1,)),
            pltpu.SemaphoreType.DMA((peers,)),
            pltpu.SemaphoreType.DMA((nsys,)),
        ],
        compiler_params=pltpu.CompilerParams(
            collective_id=0, has_side_effects=True, dimension_semantics=("arbitrary",)
        ),
    )(basis, image, selection)
    return pl.pallas_call(
        rotate_kernel,
        grid=(nsys,),
        in_specs=[whole, whole, pl.BlockSpec((1, keep, width), lambda s: (s, 0, 0))],
        out_specs=whole,
        out_shape=jax.ShapeDtypeStruct((nsys, local, width), jnp.bfloat16),
    )(basis, image, coeffs)


def solution(mesh):
    in_specs = (P(None, ("rows", "groups"), None), P(None, ("rows", "groups"), None), P())
    out_specs = P(None, ("rows", "groups"), None)
    return jax.shard_map(
        functools.partial(on_device, mesh.shape["rows"], mesh.shape["groups"]),
        mesh=mesh,
        in_specs=in_specs,
        out_specs=out_specs,
        check_vma=False,
    )
```

time: 318 us -> 68.3 us (0.21)
  other arithmetic: 118 us -> 0 us
  waiting for transfers between devices: 118 us -> 0 us
  Pallas kernels: 0 us -> 68 us
  matrix products: 44.3 us -> 0 us
  local copies, waits for them, and re-layouts: 17.2 us -> 0 us
  between operations: 14.4 us -> 0.01 us
  blocking collectives: 5.42 us -> 0 us
    another operation x25 -> x0, other arithmetic: 109 us -> none  [the longest x10 35.6 us: small_solve(): lower = jnp.linalg.cholesky(metric)]
    psum x1 -> x0, waiting for transfers between devices: 73.3 us -> none  [on_device(): summed = lax.psum(shares, 'rows')]
    pallas_call x0 -> x2, Pallas kernels: none -> 68 us  [the longest x1 54.7 us: on_device(): pl.pallas_call(functools.partial(coeff_kernel, (n_rows, n_groups), total_...]
    unnamed x3 -> x0, waiting for transfers between devices: 44.3 us -> none
    dot_general x14 -> x0, matrix products: 41.6 us -> none  [the longest x1 8.47 us: on_device(): jnp.einsum('srk,srl->skl', basis, basis, preferred_element_type=jnp.float32)]
    concatenate x1 -> x0, local copies, waits for them, and re-layouts: 11.9 us -> none  [on_device(): return jnp.concatenate([first, second], axis=2).astype(jnp.bfloat16)]
    concatenate x1 -> x0, other arithmetic: 7.8 us -> none  [on_device(): return jnp.concatenate([first, second], axis=2).astype(jnp.bfloat16)]
    all_gather x1 -> x0, blocking collectives: 5.42 us -> none  [on_device(): narrow = lax.all_gather(local_coeffs, 'groups', axis=0, tiled=True)]
  transfers between devices with their start and end apart: 2 -> 0, of which waited for: 2 -> 0; matrix products, arithmetic and copies ran while one was open for 0% -> 0% of each run, Pallas kernels for 0% -> 0%
where the time goes in v1:
time: 68.3 us; the launch traced here: 68 us
  Pallas kernels  68 us (100%)
    pallas_call x1, Pallas kernels, on_device(): pl.pallas_call(functools.partial(coeff_kernel, (n_rows, n_groups), total_...  54.7 us
    pallas_call x1, Pallas kernels, on_device(): pl.pallas_call(rotate_kernel, grid=(nsys,), in_specs=[whole, whole, pl.Bl...  13.3 us

profile of v1, /device:TPU:0, one launch (start us, length us, event | category | flops | bytes accessed | tf_op | source)
XLA Modules:
  0.0 68.0 jit_solution(7872016978367383840)
XLA Ops:
  0.0 54.7 %shard_map.37.coeffs = bf16[8,64,128]{2,1,0:T(8,128)(2,1)} custom-call(bf16[8,4096,128]{2,1,0:T(8,128)(2,1)} %basis.3, bf16[8,4096,128]{2,1,0:T(8,128)(2,1)} %image.3, s32[8,64]{1,0:T(8,128)} %chosen.1), custom_call_target="tpu_custom_call" | custom-call | tf_op jit(solution)/shard_map/pallas_call | solution.py:279
  54.7 13.3 %shard_map.38 = bf16[8,4096,128]{2,1,0:T(8,128)(2,1)} custom-call(bf16[8,4096,128]{2,1,0:T(8,128)(2,1)} %basis.3, bf16[8,4096,128]{2,1,0:T(8,128)(2,1)} %image.3, bf16[8,64,128]{2,1,0:T(8,128)(2,1)} %shard_map.37.coeffs), custom_call_target="tpu_custom_call" | custom-call | tf_op jit(solution)/shard_map/pallas_call | solution.py:301

commit v2 on v1

--- a/solution.py
+++ b/solution.py
@@ -117,26 +117,80 @@
     return gram_s, cross, gram_f
 
 
+def place_of(nsys, n_rows, n_groups):
+    inner = nsys // n_groups
+    me_r = lax.axis_index("rows")
+    me_g = lax.axis_index("groups")
+    return me_r // inner, lax.rem(me_r, inner), me_g // 2, lax.rem(me_g, 2)
+
+
+def system_at(nsys, n_rows, n_groups, step):
+    half, inner, n_x = nsys // 2, nsys // n_groups, n_groups // 2
+    z, y, x, c = place_of(nsys, n_rows, n_groups)
+    rest = lax.rem(step, half)
+    core = lax.rem(c + 1 - step // half, 2)
+    along = lax.rem(x + n_x - 1 - rest // inner, n_x)
+    row = lax.rem(y + inner - 1 - lax.rem(rest, inner), inner)
+    return core * half + along * inner + row
+
+
 def coeff_kernel(
-    sizes, total_rows, basis, image, chosen, out, shared, grams, got1, got2, got3, got4, sends, recvs, csend, crecv
+    sizes, total_rows, basis, image, chosen, out, shared, grams, got1, got2, got3, got4,
+    send1, recv1, send2, recv2, send3, recv3, send4, recv4, csend, crecv
 ):
     n_rows, n_groups = sizes
     nsys = grams.shape[0]
     width = basis.shape[2]
-    inner = nsys // n_groups
+    half, inner, n_x = nsys // 2, nsys // n_groups, n_groups // 2
     depth = n_rows // inner
-    n_x = n_groups // 2
+    late = min(2, half - 1)
     step = pl.program_id(0)
     me_r = lax.axis_index("rows")
     me_g = lax.axis_index("groups")
-    z, y = me_r // inner, lax.rem(me_r, inner)
-    x, c = me_g // 2, lax.rem(me_g, 2)
+    z, y, x, c = place_of(nsys, n_rows, n_groups)
     barrier = pltpu.get_barrier_semaphore()
     peers = n_rows * n_groups
+
+    def at(t):
+        return system_at(nsys, n_rows, n_groups, t)
 
     def nth_peer(i):
         other = lax.rem(me_r * n_groups + me_g + i, peers)
         return (other // n_groups, lax.rem(other, n_groups))
+
+    def to_core(t):
+        spot = lax.rem(at(t), half)
+        return pltpu.make_async_remote_copy(
+            src_ref=grams.at[at(t)],
+            dst_ref=got1.at[spot],
+            send_sem=send1.at[spot],
+            recv_sem=recv1.at[spot],
+            device_id=(me_r, me_g + 1 - 2 * c),
+            device_id_type=MESH,
+        )
+
+    def along_x(dx, dy):
+        spot = (dx - 1) * inner + lax.rem(y + dy, inner)
+        k = lax.rem(x + dx, n_x)
+        return pltpu.make_async_remote_copy(
+            src_ref=grams.at[c * half + k * inner + lax.rem(y + dy, inner)],
+            dst_ref=got2.at[spot],
+            send_sem=send2.at[spot],
+            recv_sem=recv2.at[spot],
+            device_id=(me_r, k * 2 + c),
+            device_id_type=MESH,
+        )
+
+    def along_rows(dy):
+        k = lax.rem(y + dy, inner)
+        return pltpu.make_async_remote_copy(
+            src_ref=grams.at[c * half + x * inner + k],
+            dst_ref=got3.at[dy - 1],
+            send_sem=send3.at[dy - 1],
+            recv_sem=recv3.at[dy - 1],
+            device_id=(z * inner + k, me_g),
+            device_id_type=MESH,
+        )
 
     @pl.when(step == 0)
     def _():
@@ -149,43 +203,47 @@
     both = jnp.concatenate([basis[0], image[0]], axis=1)
     gram = lax.dot_general(both, both, TN, preferred_element_type=jnp.float32)
     cross, mixed, diag = pack(gram, width)
-    grams[step, 0:width, :] = cross
-    grams[step, width : 2 * width, :] = mixed
-    grams[step, 2 * width :, :] = diag
+    now = at(step)
+    grams[now, 0:width, :] = cross
+    grams[now, width : 2 * width, :] = mixed
+    grams[now, 2 * width :, :] = diag
+
+    @pl.when(step == late)
+    def _():
+        pl.semaphore_wait(barrier, peers - 1)
+        for t in range(late + 1):
+            to_core(t).start()
+
+    @pl.when(jnp.logical_and(step > late, step < half))
+    def _():
+        to_core(step).start()
+
+    for t in range(half, nsys):
+
+        @pl.when(step == t)
+        def _():
+            own = at(t)
+            spot = lax.rem(own, half)
+            to_core(t).wait_recv()
+            grams[own] += got1[spot]
+            dx = n_x - 1 - (t - half) // inner
+            if dx:
+                along_x(dx, inner - 1 - (t - half) % inner).start()
 
     @pl.when(step == nsys - 1)
     def _():
-        pl.semaphore_wait(barrier, peers - 1)
-        base = 0
-        count = nsys
-        slot = 0
-        for size, at, spot, got in (
-            (2, c, lambda k: (me_r, me_g + k - c), got1),
-            (n_x, x, lambda k: (me_r, me_g + 2 * (k - x)), got2),
-            (inner, y, lambda k: (me_r + k - y, me_g), got3),
-        ):
-            if size == 1:
-                continue
-            count = count // size
-            copies = []
-            for d in range(1, size):
-                k = lax.rem(at + d, size)
-                copy = pltpu.make_async_remote_copy(
-                    src_ref=grams.at[pl.ds(base + k * count, count)],
-                    dst_ref=got.at[pl.ds((d - 1) * count, count)],
-                    send_sem=sends.at[slot],
-                    recv_sem=recvs.at[slot],
-                    device_id=spot(k),
-                    device_id_type=MESH,
-                )
-                copy.start()
-                copies.append(copy)
-                slot += 1
-            base = base + at * count
-            for d, copy in enumerate(copies):
-                copy.wait()
-                grams[pl.ds(base, count)] += got[pl.ds(d * count, count)]
-        mine = base
+        base = c * half + x * inner
+        for dy in reversed(range(inner)):
+            k = lax.rem(y + dy, inner)
+            for dx in range(1, n_x):
+                along_x(dx, dy).wait_recv()
+                grams[base + k] += got2[(dx - 1) * inner + k]
+            if dy:
+                along_rows(dy).start()
+        mine = base + y
+        for dy in range(1, inner):
+            along_rows(dy).wait_recv()
+            grams[mine] += got3[dy - 1]
         root = lax.rem(2 * c + x + y, depth)
 
         @pl.when(z != root)
@@ -193,8 +251,8 @@
             copy = pltpu.make_async_remote_copy(
                 src_ref=grams.at[mine],
                 dst_ref=got4.at[lax.rem(z - root + depth, depth) - 1],
-                send_sem=sends.at[slot],
-                recv_sem=recvs.at[slot + lax.rem(z - root + depth, depth) - 1],
+                send_sem=send4.at[0],
+                recv_sem=recv4.at[lax.rem(z - root + depth, depth) - 1],
                 device_id=(root * inner + y, me_g),
                 device_id_type=MESH,
             )
@@ -208,8 +266,8 @@
                 pltpu.make_async_remote_copy(
                     src_ref=grams.at[mine],
                     dst_ref=got4.at[k],
-                    send_sem=sends.at[slot],
-                    recv_sem=recvs.at[slot + k],
+                    send_sem=send4.at[0],
+                    recv_sem=recv4.at[k],
                     device_id=(me_r, me_g),
                     device_id_type=MESH,
                 ).wait_recv()
@@ -255,14 +313,25 @@
                     device_id_type=MESH,
                 ).wait_recv()
 
+        for t in range(half):
+            to_core(t).wait_send()
+        for dy in range(inner):
+            for dx in range(1, n_x):
+                along_x(dx, dy).wait_send()
+            if dy:
+                along_rows(dy).wait_send()
         out[...] = shared[...]
 
 
 def rotate_kernel(basis, image, coeffs, out):
     narrow = coeffs[0]
-    first = lax.dot_general(basis[0], narrow, NT, preferred_element_type=jnp.float32)
-    second = lax.dot_general(image[0], narrow, NT, preferred_element_type=jnp.float32)
-    out[0] = jnp.concatenate([first, second], axis=1).astype(out.dtype)
+    empty = jnp.zeros_like(narrow)
+    upper = jnp.concatenate([narrow, empty], axis=1)
+    lower = jnp.concatenate([empty, narrow], axis=1)
+    both = jnp.concatenate([basis[0], image[0]], axis=1)
+    twice = jnp.concatenate([upper, lower], axis=0)
+    turned = lax.dot_general(both, twice, NT, preferred_element_type=jnp.float32)
+    out[0] = turned.astype(out.dtype)
 
 
 def on_device(n_rows, n_groups, basis, image, selection):
@@ -273,13 +342,15 @@
     inner = nsys // n_groups
     depth = n_rows // inner
     n_x = n_groups // 2
-    hops = n_x + max(inner - 1, 1)
     tall = 2 * width + 8
     whole = pl.BlockSpec((1, local, width), lambda s: (s, 0, 0))
+    ordered = pl.BlockSpec(
+        (1, local, width), lambda s: (system_at(nsys, n_rows, n_groups, s), 0, 0)
+    )
     coeffs = pl.pallas_call(
         functools.partial(coeff_kernel, (n_rows, n_groups), total_rows),
         grid=(nsys,),
-        in_specs=[whole, whole, pl.BlockSpec(memory_space=pltpu.VMEM)],
+        in_specs=[ordered, ordered, pl.BlockSpec(memory_space=pltpu.VMEM)],
         out_specs=pl.BlockSpec(memory_space=pltpu.VMEM),
         out_shape=jax.ShapeDtypeStruct((nsys, keep, width), jnp.bfloat16),
         scratch_shapes=[
@@ -289,8 +360,14 @@
             pltpu.VMEM(((n_x - 1) * nsys // n_groups, tall, width), jnp.float32),
             pltpu.VMEM((max(inner - 1, 1), tall, width), jnp.float32),
             pltpu.VMEM((depth - 1, tall, width), jnp.float32),
-            pltpu.SemaphoreType.DMA((hops + 1,)),
-            pltpu.SemaphoreType.DMA((hops + depth - 1,)),
+            pltpu.SemaphoreType.DMA((nsys // 2,)),
+            pltpu.SemaphoreType.DMA((nsys // 2,)),
+            pltpu.SemaphoreType.DMA(((n_x - 1) * inner,)),
+            pltpu.SemaphoreType.DMA(((n_x - 1) * inner,)),
+            pltpu.SemaphoreType.DMA((max(inner - 1, 1),)),
+            pltpu.SemaphoreType.DMA((max(inner - 1, 1),)),
+            pltpu.SemaphoreType.DMA((1,)),
+            pltpu.SemaphoreType.DMA((depth - 1,)),
             pltpu.SemaphoreType.DMA((peers,)),
             pltpu.SemaphoreType.DMA((nsys,)),
         ],

time: 68.3 us -> 60.1 us (0.88)
  Pallas kernels: 68 us -> 59.8 us
    pallas_call x1, Pallas kernels: 54.7 us -> 46.7 us  [on_device(): pl.pallas_call(functools.partial(coeff_kernel, (n_rows, n_groups), total_...]
where the time goes in v2:
time: 60.1 us; the launch traced here: 59.8 us
  Pallas kernels  59.8 us (100%)
    pallas_call x1, Pallas kernels, on_device(): pl.pallas_call(functools.partial(coeff_kernel, (n_rows, n_groups), total_...  46.7 us
    pallas_call x1, Pallas kernels, on_device(): pl.pallas_call(rotate_kernel, grid=(nsys,), in_specs=[whole, whole, pl.Bl...  13 us

profile of v2, /device:TPU:0, one launch (start us, length us, event | category | flops | bytes accessed | tf_op | source)
XLA Modules:
  0.0 59.8 jit_solution(1561562468818190761)
XLA Ops:
  0.0 46.7 %shard_map.37.coeffs = bf16[8,64,128]{2,1,0:T(8,128)(2,1)} custom-call(bf16[8,4096,128]{2,1,0:T(8,128)(2,1)} %basis.3, bf16[8,4096,128]{2,1,0:T(8,128)(2,1)} %image.3, s32[8,64]{1,0:T(8,128)} %chosen.1), custom_call_target="tpu_custom_call" | custom-call | tf_op jit(solution)/shard_map/pallas_call | solution.py:350
  46.7 13.0 %shard_map.38 = bf16[8,4096,128]{2,1,0:T(8,128)(2,1)} custom-call(bf16[8,4096,128]{2,1,0:T(8,128)(2,1)} %basis.3, bf16[8,4096,128]{2,1,0:T(8,128)(2,1)} %image.3, bf16[8,64,128]{2,1,0:T(8,128)(2,1)} %shard_map.37.coeffs), custom_call_target="tpu_custom_call" | custom-call | tf_op jit(solution)/shard_map/pallas_call | solution.py:378
